TPU v7x, 32 devices: a 4x4x1 block of a 4x4x8 slice. The times are simulated.
32 devices in a mesh: rep: 2 (over z, core), dp: 16 (over x, y).
Axes of the slice: x: 4, y: 4, z: 1, core: 2. Of those that a mesh axis runs over, the one named last changes fastest.
The devices are a block of a 4x4x8 slice.
Arguments:
- g_w_gate: bfloat16 [32, 2, 1024, 3328], P(('rep', 'dp')), parts along dimension 0
- g_w_up: bfloat16 [32, 2, 1024, 3328], P(('rep', 'dp')), parts along dimension 0
- g_w_down: bfloat16 [32, 2, 3328, 1024], P(('rep', 'dp')), parts along dimension 0
- w_gate: bfloat16 [2, 1024, 3328], replicated
- w_up: bfloat16 [2, 1024, 3328], replicated
- w_down: bfloat16 [2, 3328, 1024], replicated
- m_w_gate: float32 [2, 1024, 3328], P(None, 'dp')
- m_w_up: float32 [2, 1024, 3328], P(None, 'dp')
- m_w_down: float32 [2, 3328, 1024], P(None, 'dp')
- v_w_gate: float32 [2, 1024, 3328], P(None, 'dp')
- v_w_up: float32 [2, 1024, 3328], P(None, 'dp')
- v_w_down: float32 [2, 3328, 1024], P(None, 'dp')
Outputs:
- output 1: bfloat16 [4, 1024, 3328], P('rep'), parts along dimension 0
- output 2: bfloat16 [4, 1024, 3328], P('rep'), parts along dimension 0
- output 3: bfloat16 [4, 3328, 1024], P('rep'), parts along dimension 0
- output 4: float32 [4, 1024, 3328], P('rep', 'dp'), parts along dimension 0
- output 5: float32 [4, 1024, 3328], P('rep', 'dp'), parts along dimension 0
- output 6: float32 [4, 3328, 1024], P('rep', 'dp'), parts along dimension 0
- output 7: float32 [4, 1024, 3328], P('rep', 'dp'), parts along dimension 0
- output 8: float32 [4, 1024, 3328], P('rep', 'dp'), parts along dimension 0
- output 9: float32 [4, 3328, 1024], P('rep', 'dp'), parts along dimension 0
There are 2 independent parts. A program takes and returns all parts, laid end to end along the dimension named above; an argument that names none is the same for every part.
All inputs are finite; a program needn't handle non-finite values.
Results may differ from a plain program's by a relative error of at most 0.022.
Values are sent between devices in bfloat16 or wider.
A program may use at most 768 MiB of HBM per device.

v0:
```python
import functools
import math

import jax
import jax.numpy as jnp
from jax import lax
from jax.experimental import pallas as pl
from jax.experimental.pallas import tpu as pltpu
from jax.sharding import PartitionSpec as P

MESH = pl.DeviceIdType.MESH
ROWS, COLS = 16, 256
LIMIT = 67043328
FAR, NEAR, FAR2, LAST, PARTS, ON, REST = 0, 2, 4, 5, 6, 9, 11
BLOCKS = (2, 2, 2, 4, 1, 4, 1, 1, 1, 2, 2, 8)


def adamw(w, m, v, g):
    m = 0.9 * m + 0.1 * g
    v = 0.95 * v + 0.05 * g * g
    step = m * lax.rsqrt(v + 1e-8) + 0.1 * w
    return (w - 0.02 * step).astype(jnp.bfloat16), m, v


def kernel(side, *refs):
    terms, weights, ms, vs = (refs[i : i + 3] for i in range(0, 12, 3))
    outs, staged, gs = refs[12:14], refs[14:18], refs[18:21]
    own, first, second, wide, narrow = (refs[i : i + 3] for i in range(21, 36, 3))
    recv_sem, (send_sem, load_sem, moment_sem, store_sem) = refs[36:39], refs[39:43]

    me = lax.axis_index("dp")
    x, y = me // side, me % side
    for neighbour in ((x + 1) % side * side + y, (x + side - 1) % side * side + y, x * side + (y + 1) % side, x * side + (y + side - 1) % side):
        pl.semaphore_signal(pltpu.get_barrier_semaphore(), inc=1, device_id={"dp": neighbour}, device_id_type=MESH)
    pl.semaphore_wait(pltpu.get_barrier_semaphore(), 4)

    def place(layer):
        return x * (1 - layer) + y * layer, x * layer + y * (1 - layer)

    def index(layer, p, q):
        return (p + 2 * side) % side * (side * (1 - layer) + layer) + (q + 2 * side) % side * (1 - layer + side * layer)

    def to(layer, ring, by):
        p, q = place(layer)
        return {"dp": index(layer, p + by, q) if ring == 0 else index(layer, p, q + by)}

    def part(w, half):
        size = own[w].shape[2]
        cut = (size // ROWS + 1) // 2 * ROWS
        return (pl.ds(0, cut), pl.ds(cut, size - cut), pl.ds(0, size))[half]

    def rows(w, layer, p, q, half=2):
        inside = part(w, half)
        return pl.ds(pl.multiple_of(index(layer, p, q) * own[w].shape[2] + inside.start, ROWS), inside.size)

    def send(w, layer, leg, group, source, target, device):
        pltpu.make_async_remote_copy(source, target, send_sem.at[w, leg], recv_sem[w].at[layer, group], device_id=device, device_id_type=MESH).start()

    def take(ref, sem):
        pltpu.make_async_copy(ref, ref, sem).wait()

    def wait(w, layer, group, blocks=None):
        take(own[w].at[layer, pl.ds(0, blocks or BLOCKS[group])] if isinstance(group, int) else own[w].at[layer, pl.ds(0, blocks)], recv_sem[w].at[layer, group])

    def home(w, layer, d, half=2):
        p, q = place(layer)
        return staged[2 * layer + 1 - d % 2].at[d % side // 2, part(w, half)] if w == 2 else outs[w].at[layer, rows(w, layer, p, q + d, half)]

    def home_there(w, layer, d, by, half=2):
        return home(w, layer, (d - by) % side if w == 2 else d, half)

    def over_layers(f, times=1, unroll=False):
        if unroll:
            for n in range(2):
                f(n)
            return

        def body(n, _):
            f(n % 2, n // 2) if times > 1 else f(n)
            return 0

        lax.fori_loop(0, 2 * times, body, 0)

    def blockwise(w, half, f):
        inside = part(w, half)

        def body(r, _):
            at = pl.ds(pl.multiple_of(inside.start + r * ROWS, ROWS), ROWS)
            for c in range(0, own[w].shape[3], COLS):
                f(at, pl.ds(c, COLS))
            return 0

        lax.fori_loop(0, inside.size // ROWS, body, 0)

    def add(w, layer, half, slot, *others):
        def one(at, c):
            total = own[w][layer, slot, at, c].astype(jnp.float32)
            for ref, other in others:
                total += ref[layer, other, at, c].astype(jnp.float32)
            own[w][layer, slot, at, c] = total.astype(jnp.bfloat16)

        blockwise(w, half, one)


    def loads(w):
        def f(layer):
            p, q = place(layer)
            for slot, (far, d) in enumerate(((1, 2), (1, 1), (-1, 3), (-1, 0), (0, 0), (0, 1), (0, 2), (0, 3))):
                pltpu.make_async_copy(terms[w].at[0, layer, rows(w, layer, p + far, q + d)], own[w].at[layer, slot], load_sem.at[w]).start()

        over_layers(f)

    def raw1(w):
        def f(layer, i):
            p, q = place(layer)
            for k, d, by in ((0, 2 - i, 1), (2, 3 - 3 * i, -1)):
                source = terms[w].at[0, layer, rows(w, layer, p + 2, q + d)]
                send(w, layer, 0, FAR + i, source, first[w].at[layer, k + i], to(layer, 0, by))

        def g(layer, i):
            p, q = place(layer)
            for k, d, by, group in ((4, 3 - 3 * i, 1, NEAR + 1 + 2 * i), (6, 2 - i, -1, NEAR + i)):
                source = terms[w].at[0, layer, rows(w, layer, p + by, q + d)]
                send(w, layer, 0, group, source, first[w].at[layer, k + i], to(layer, 0, by))

        over_layers(f, 2)
        over_layers(g, 2)

    def fwd1(w):
        take(own[w], load_sem.at[w])
        for i in range(2):

            def f(layer, i=i):
                wait(w, layer, FAR + i)
                for k, by, group in ((0, 1, NEAR + i), (2, -1, NEAR + 1 + 2 * i)):
                    add(w, layer, 2, k + i, (first[w], k + i))
                    send(w, layer, 0, group, own[w].at[layer, k + i], first[w].at[layer, 8 + k + i], to(layer, 0, by))

            over_layers(f)

    def send2(w, layer, slot, half, group, target, by):
        at = part(w, half)
        send(w, layer, 1, group, own[w].at[layer, slot, at], second[w].at[layer, target, at], to(layer, 1, by))

    def raw2(w):
        def f(layer):
            wait(w, layer, NEAR)
            add(w, layer, 2, 6, (first[w], 8), (first[w], 6))
            send2(w, layer, 6, 0, FAR2, 0, 1)
            send2(w, layer, 6, 1, FAR2, 0, -1)

        def g(layer):
            wait(w, layer, NEAR + 1)
            add(w, layer, 1, 5, (first[w], 9), (first[w], 7))
            send2(w, layer, 5, 1, LAST, 1, 1)
            add(w, layer, 0, 7, (first[w], 4), (first[w], 10))
            send2(w, layer, 7, 0, LAST, 2, -1)

        over_layers(f)
        over_layers(g)

    def fwd2(w):
        def f(layer):
            wait(w, layer, FAR2)
            add(w, layer, 0, 5, (first[w], 9), (first[w], 7), (second[w], 0))
            send2(w, layer, 5, 0, LAST, 1, 1)
            add(w, layer, 1, 7, (first[w], 4), (first[w], 10), (second[w], 0))
            send2(w, layer, 7, 1, LAST, 2, -1)

        over_layers(f)

    def load_moments(w, layer):
        p, q = place(layer)
        slot = layer if w < 2 else 0
        pltpu.make_async_copy(ms[w].at[layer], wide[w].at[slot, 0], moment_sem.at[w, 0]).start()
        pltpu.make_async_copy(vs[w].at[layer], wide[w].at[slot, 1], moment_sem.at[w, 0]).start()
        pltpu.make_async_copy(weights[w].at[layer, rows(w, layer, p, q)], narrow[w].at[slot], moment_sem.at[w, 1]).start()

    def take_moments(w):
        take(wide[w], moment_sem.at[w, 0])
        take(narrow[w], moment_sem.at[w, 1])

    def step(w):
        if w < 2:
            take_moments(w)

        def f(layer):
            slot = layer if w < 2 else 0
            if w == 2:
                load_moments(w, layer)
            wait(w, layer, LAST)
            if w == 2:
                take_moments(w)

            def one(at, c):
                total = own[w][layer, 4, at, c].astype(jnp.float32)
                for ref, other in ((first[w], 5), (first[w], 11), (second[w], 1), (second[w], 2)):
                    total += ref[layer, other, at, c].astype(jnp.float32)
                g = total.astype(jnp.bfloat16)
                own[w][layer, 4, at, c] = g
                old = narrow[w][slot, at, c].astype(jnp.float32)
                second[w][layer, 1, at, c] = adamw(old, wide[w][slot, 0, at, c], wide[w][slot, 1, at, c], g.astype(jnp.float32))[0]

            blockwise(w, 2, one)
            for group, half, by in ((PARTS, 1, 1), (PARTS, 0, -1), (PARTS + 1, 0, 1), (PARTS + 1, 1, -1)):
                source = second[w].at[layer, 1, part(w, half)]
                send(w, layer, 2, group, source, home_there(w, layer, 0, by, half), to(layer, 1, by))
            pltpu.make_async_copy(own[w].at[layer, 4], gs[w].at[layer], store_sem.at[w, 0]).start()
            pltpu.make_async_copy(second[w].at[layer, 1], home(w, layer, 0), store_sem.at[w, 1]).start()

        over_layers(f, unroll=w == 2)

    def gather2(w):
        def f(layer):
            wait(w, layer, PARTS)
            for half, by in ((1, 1), (0, -1)):
                send(w, layer, 2, PARTS + 2, home(w, layer, -by, half), home_there(w, layer, -by, by, half), to(layer, 1, by))

        over_layers(f, unroll=w == 2)

    def give(w, layer, d, source=None):
        source = home(w, layer, d) if source is None else source
        for by in (1, -1):
            on = (by == 1) == (d % 2 == 0)
            if w < 2:
                send(w, layer, 3, ON + d // 2 if on else REST, source, home(w, layer, d), to(layer, 0, by))
            elif on:
                send(w, layer, 3, REST, source, staged[2 * layer + d % 2].at[2 + d // 2], to(layer, 0, by))

    def gather1(w):
        def f(layer):
            give(w, layer, 0, second[w].at[layer, 1])
            wait(w, layer, PARTS + 1)
            give(w, layer, 1)
            give(w, layer, 3)

        over_layers(f, unroll=w == 2)

    def gather1_far(w):
        def f(layer):
            wait(w, layer, PARTS + 2)
            give(w, layer, 2)

        over_layers(f, unroll=w == 2)

    def gather1_on(w):
        def f(layer, i):
            p, q = place(layer)
            wait(w, layer, ON + i, 2)
            for d, by in ((2 * i, 1), (1 + 2 * i, -1)):
                at = outs[w].at[layer, rows(w, layer, p - by, q + d)]
                send(w, layer, 3, REST, at, at, to(layer, 0, by))

        over_layers(f, 2)

    def finish(w):
        for layer in range(2):
            wait(w, layer, REST, 4 if w == 2 else 8)
        for leg, ref in enumerate((first[w], second[w], second[w], own[w].at[0] if w == 2 else first[w])):
            take(ref, send_sem.at[w, leg])
        for n in range(2):
            take(gs[w], store_sem.at[w, n])

    raw1(0)
    loads(0)
    over_layers(lambda layer: load_moments(0, layer))
    loads(1)
    fwd1(0)
    raw1(1)
    loads(2)
    raw2(0)
    fwd1(1)
    raw1(2)
    fwd2(0)
    raw2(1)
    fwd1(2)
    step(0)
    over_layers(lambda layer: load_moments(1, layer))
    fwd2(1)
    raw2(2)
    gather2(0)
    gather1(0)
    step(1)
    fwd2(2)
    gather1_far(0)
    gather2(1)
    gather1(1)
    step(2)
    gather1_on(0)
    gather1_far(1)
    gather2(2)
    gather1(2)
    gather1_on(1)
    gather1_far(2)
    for w in range(3):
        finish(w)


def spots(side, size, shift):
    me = lax.axis_index("dp")
    for layer in range(2):
        for way in range(2):
            for slot in range(side):
                far = (2 * way - 1) * (shift + slot // 2)
                d = (1 - way + slot // 2) % 2 + 2 * (slot % 2)
                a, b = (far, d) if layer == 0 else (d, far)
                block = (me // side + a + side) % side * side + (me % side + b + side) % side
                yield layer, way, slot, pl.ds(pl.multiple_of(block * size, ROWS), size)


def settle(side, *refs):
    gs, ms, vs, outs, staged = refs[:3], refs[3:6], refs[6:9], refs[9:11], refs[11:15]
    new_ms, new_vs, wholes = refs[15:18], refs[18:21], refs[21:24]
    g_at, m_at, v_at, w_at = refs[24:27], refs[27:30], refs[30:33], refs[33:36]
    moment_sem, store_sem, *copy_sem = refs[36:41]

    copies = []
    for w in range(2):
        pieces, size = w_at[w].shape[1:3]
        for layer in range(2):
            for n in range(pieces):
                at = pl.ds(n * size, size)
                copies.append((outs[w].at[layer, at], w_at[w].at[layer, n], wholes[w].at[layer, at], copy_sem[w].at[layer, n]))
    for layer, way, slot, at in spots(side, w_at[2].shape[2], 0):
        n = way * side + slot
        copies.append((staged[2 * layer + way].at[slot], w_at[2].at[layer, n], wholes[2].at[layer, at], copy_sem[2].at[layer, n]))

    for w in range(3):
        for n, (source, target) in enumerate(((gs, g_at), (ms, m_at), (vs, v_at))):
            pltpu.make_async_copy(source[w], target[w], moment_sem.at[w, n]).start()
    for source, buffer, _, sem in copies:
        pltpu.make_async_copy(source, buffer, sem).start()
    stores = []
    for w in range(3):
        for n, (source, target) in enumerate(((gs, g_at), (ms, m_at), (vs, v_at))):
            pltpu.make_async_copy(source[w], target[w], moment_sem.at[w, n]).wait()

        def body(r, _, w=w):
            for layer in range(2):
                at = pl.ds(pl.multiple_of(r * ROWS, ROWS), ROWS)
                for c in range(0, m_at[w].shape[2], COLS):
                    here = (layer, at, pl.ds(c, COLS))
                    _, m_at[w][here], v_at[w][here] = adamw(0.0, m_at[w][here], v_at[w][here], g_at[w][here].astype(jnp.float32))
            return 0

        lax.fori_loop(0, m_at[w].shape[1] // ROWS, body, 0)
        stores += [pltpu.make_async_copy(a[w], b[w], store_sem.at[w, n]) for n, (a, b) in enumerate(((m_at, new_ms), (v_at, new_vs)))]
        stores[-2].start()
        stores[-1].start()
    for source, buffer, target, sem in copies:
        pltpu.make_async_copy(source, buffer, sem).wait()
        stores.append(pltpu.make_async_copy(buffer, target, sem))
        stores[-1].start()
    for copy in stores:
        copy.wait()


def patch(side, layer, *refs):
    brought, whole, sem = refs[1:3], refs[3], refs[4]
    moves = []
    for here, way, slot, at in spots(side, brought[0].shape[1], 1):
        if here == layer:
            moves.append(pltpu.make_async_copy(brought[way].at[slot], whole.at[layer, at], sem.at[way, slot]))
            moves[-1].start()
    for move in moves:
        move.wait()


def solution(mesh):
    side = math.isqrt(mesh.shape["dp"])

    def on(ring, by):
        return [(x * side + y, (x + by) % side * side + y if ring == 0 else x * side + (y + by) % side) for x in range(side) for y in range(side)]

    def step(*arrays):
        weights, m, v = (arrays[i : i + 3] for i in (3, 6, 9))
        blocks = [one.shape[1:] for one in m]
        layers = m[0].shape[0]
        bf16, f32, dma = jnp.bfloat16, jnp.float32, pltpu.SemaphoreType.DMA
        anywhere = pl.BlockSpec(memory_space=pl.ANY)

        def call(f, name, inputs, outputs, scratch, params, held=0, limit=LIMIT, **more):
            return pl.pallas_call(
                f,
                out_shape=[jax.ShapeDtypeStruct(one.shape, one.dtype) for one in outputs],
                in_specs=[anywhere] * (len(inputs) - held) + [pl.BlockSpec(memory_space=pltpu.VMEM)] * held,
                out_specs=[anywhere] * len(outputs),
                scratch_shapes=scratch,
                compiler_params=pltpu.CompilerParams(vmem_limit_bytes=limit, **params),
                name=name,
                **more,
            )(*inputs)

        scratch = [pltpu.VMEM((layers, count, *b), bf16) for count in (8, 12, 3) for b in blocks]
        scratch += [pltpu.VMEM((k, 2, *blocks[w]), f32) for w, k in ((0, layers), (2, 1))]
        scratch += [pltpu.VMEM((k, *blocks[w]), bf16) for w, k in ((0, layers), (2, 1))]
        scratch += [dma((layers, len(BLOCKS)))] * 3 + [dma((3, 4)), dma((3,)), dma((3, 2)), dma((3, 2))]

        def exchange(*refs):
            head, (wide, wide2, narrow, narrow2), sems = refs[:30], refs[30:34], refs[34:]
            kernel(side, *head, wide, wide, wide2, narrow, narrow, narrow2, *sems)

        stage = jax.ShapeDtypeStruct((side, *blocks[2]), bf16)
        g = [jax.ShapeDtypeStruct(one.shape, bf16) for one in m]
        result = call(exchange, "exchange", arrays, [*weights[:2], *[stage] * 4, *g], scratch, {"collective_id": 0, "has_side_effects": True})
        whole, staged, g = result[:2], result[2:6], result[6:]
        brought = [lax.ppermute(one, "dp", on(n // 2, 1 - n % 2 * 2)) for n, one in enumerate(staged)]

        copied = [(layers, side, w.shape[1] // side, w.shape[2]) for w in weights[:2]] + [(layers, 2 * side, *blocks[2])]
        scratch = [pltpu.VMEM(one.shape, t) for t in (bf16, f32, f32) for one in m] + [pltpu.VMEM(shape, bf16) for shape in copied]
        scratch += [dma((3, 3)), dma((3, 2))] + [dma(shape[:2]) for shape in copied]
        cost = pl.CostEstimate(flops=18 * m[0].size, bytes_accessed=5 * weights[0].size, transcendentals=0)
        result = call(functools.partial(settle, side), "settle", [*g, *m, *v, *whole, *staged], [*m, *v, *weights], scratch, {}, limit=LIMIT * 8 // 9, cost_estimate=cost)
        *moments, gate, up, down = result
        few = {"held": 2, "limit": LIMIT // 8, "input_output_aliases": {0: 0}}
        for layer in range(layers):
            inputs = [down, *brought[2 * layer : 2 * layer + 2]]
            (down,) = call(functools.partial(patch, side, layer), "patch", inputs, [down], [dma((2, side))], {}, **few)
        return (gate, up, down, *moments)

    all_of, cut = P(None, None, None), P(None, "dp", None)
    return jax.shard_map(
        step,
        mesh=mesh,
        in_specs=(P(("rep", "dp"), None, None, None),) * 3 + (all_of,) * 3 + (cut,) * 6,
        out_specs=(P("rep", None, None),) * 3 + (P("rep", "dp", None),) * 6,
        check_vma=False,
    )
```

profile of v0, /device:TPU:97, one launch (start us, length us, event | category | flops | bytes accessed | tf_op | source)
XLA Modules:
  0.0 426.9 jit_solution(10538024755232352953)
XLA Ops:
  0.6 383.6 %exchange.1 = (bf16[2,1024,3328]{2,1,0:T(8,128)(2,1)}, bf16[2,1024,3328]{2,1,0:T(8,128)(2,1)}, bf16[4,208,1024]{2,1,0:T(8,128)(2,1)}, bf16[4,208,1024]{2,1,0:T(8...) custom-call(bf16[1,2,1024,3328]{3,2,1,0:T(8,128)(2,1)} %refs_0_.1, ...), custom_call_target="tpu_custom_call" | custom-call | tf_op jit(solution)/shard_map/exchange/pallas_call | solution.py:383
  384.3 0.1 collective-permute-start
  384.4 2.7 collective-permute-start.1
  387.1 0.0 collective-permute-start.2
  387.1 2.7 collective-permute-start.3
  389.7 29.7 %settle.1 = (f32[2,64,3328]{2,1,0:T(8,128)}, f32[2,64,3328]{2,1,0:T(8,128)}, f32[2,208,1024]{2,1,0:T(8,128)}, f32[2,64,3328]{2,1,0:T(8,128)}, f32[2,64,3328]{2,1...) custom-call(bf16[2,64,3328]{2,1,0:T(8,128)(2,1)} %get-tuple-element., ...), custom_call_target="tpu_custom_call" | custom-call | flops 7667712 | bytes 34078720 | tf_op jit(solution)/shard_map/settle/pallas_call | solution.py:383
  419.5 3.5 collective-permute-done.refs_1_
  423.0 0.0 collective-permute-done.1.refs_2_
  423.0 1.8 patch.2.refs_0_
  424.8 0.3 collective-permute-done.2.refs_1_
  425.1 0.0 collective-permute-done.3.refs_2_
  425.1 1.8 patch.3
Async XLA Ops:
  384.3 38.7 %collective-permute-start = (bf16[4,208,1024]{2,1,0:T(8,128)(2,1)}, bf16[4,208,1024]{2,1,0:T(8,128)(2,1)S(1)}, u32[]{:S(2)}, u32[]{:S(2)}) collective-permute-start(bf16[4,208,1024]{2,1,0:T(8,128)(2,1)} %get-tuple-element.32.refs_11_), channel_id=1, source_target_pairs={{0,4},{1,5},{2,6},{3,7},{4,8},{5,9},{6,10},{7,11},{8,12},{9,13},{1... | collective-permute-start | bytes 5111816 | tf_op jit(solution)/shard_map/ppermute | solution.py:407
  384.4 38.6 %collective-permute-start.1 = (bf16[4,208,1024]{2,1,0:T(8,128)(2,1)}, bf16[4,208,1024]{2,1,0:T(8,128)(2,1)S(1)}, u32[]{:S(2)}, u32[]{:S(2)}) collective-permute-start(bf16[4,208,1024]{2,1,0:T(8,128)(2,1)} %get-tuple-element.33.refs_12_), channel_id=1, source_target_pairs={{0,12},{1,13},{2,14},{3,15},{4,0},{5,1},{6,2},{7,3},{8,4},{9,5},{1... | collective-permute-start | bytes 5111816 | tf_op jit(solution)/shard_map/ppermute | solution.py:407
  387.1 38.1 %collective-permute-start.2 = (bf16[4,208,1024]{2,1,0:T(8,128)(2,1)}, bf16[4,208,1024]{2,1,0:T(8,128)(2,1)S(1)}, u32[]{:S(2)}, u32[]{:S(2)}) collective-permute-start(bf16[4,208,1024]{2,1,0:T(8,128)(2,1)} %get-tuple-element.34.refs_13_), channel_id=1, source_target_pairs={{0,1},{1,2},{2,3},{3,0},{4,5},{5,6},{6,7},{7,4},{8,9},{9,10},{10,1... | collective-permute-start | bytes 5111816 | tf_op jit(solution)/shard_map/ppermute | solution.py:407
  387.1 38.1 %collective-permute-start.3 = (bf16[4,208,1024]{2,1,0:T(8,128)(2,1)}, bf16[4,208,1024]{2,1,0:T(8,128)(2,1)S(1)}, u32[]{:S(2)}, u32[]{:S(2)}) collective-permute-start(bf16[4,208,1024]{2,1,0:T(8,128)(2,1)} %get-tuple-element.35.refs_14_), channel_id=1, source_target_pairs={{0,3},{1,0},{2,1},{3,2},{4,7},{5,4},{6,5},{7,6},{8,11},{9,8},{10,9... | collective-permute-start | bytes 5111816 | tf_op jit(solution)/shard_map/ppermute | solution.py:407
where the time goes:
time: 428 us; the launch traced here: 427 us
  Pallas kernels  417 us (97%)
  starting transfers between devices  5.43 us (1%)
    pallas_call x4, Pallas kernels, call(): pl.pallas_call(f, out_shape=[jax.ShapeDtypeStruct(one.shape, one.dtype) f...  417 us
  transfers between devices with their start and end apart: 4, of which 2 were waited for; matrix products, arithmetic and copies ran while one was open for 0% of the time, Pallas kernels for 7%

commit v1 on v0

--- a/solution.py
+++ b/solution.py
@@ -8,6 +8,7 @@
 from jax.experimental.pallas import tpu as pltpu
 from jax.sharding import PartitionSpec as P
 
+
 MESH = pl.DeviceIdType.MESH
 ROWS, COLS = 16, 256
 LIMIT = 67043328
@@ -26,7 +27,7 @@
     terms, weights, ms, vs = (refs[i : i + 3] for i in range(0, 12, 3))
     outs, staged, gs = refs[12:14], refs[14:18], refs[18:21]
     own, first, second, wide, narrow = (refs[i : i + 3] for i in range(21, 36, 3))
-    recv_sem, (send_sem, load_sem, moment_sem, store_sem) = refs[36:39], refs[39:43]
+    recv_sem, send_sem, load_sem, moment_sem, store_sem = refs[36:41]
 
     me = lax.axis_index("dp")
     x, y = me // side, me % side
@@ -53,14 +54,14 @@
         inside = part(w, half)
         return pl.ds(pl.multiple_of(index(layer, p, q) * own[w].shape[2] + inside.start, ROWS), inside.size)
 
-    def send(w, layer, leg, group, source, target, device):
-        pltpu.make_async_remote_copy(source, target, send_sem.at[w, leg], recv_sem[w].at[layer, group], device_id=device, device_id_type=MESH).start()
+    def send(w, leg, group, source, target, device):
+        pltpu.make_async_remote_copy(source, target, send_sem.at[w, leg], recv_sem.at[w, group], device_id=device, device_id_type=MESH).start()
 
     def take(ref, sem):
         pltpu.make_async_copy(ref, ref, sem).wait()
 
-    def wait(w, layer, group, blocks=None):
-        take(own[w].at[layer, pl.ds(0, blocks or BLOCKS[group])] if isinstance(group, int) else own[w].at[layer, pl.ds(0, blocks)], recv_sem[w].at[layer, group])
+    def wait(w, group, blocks=None):
+        take(own[w].at[:, pl.ds(0, blocks or BLOCKS[group])], recv_sem.at[w, group])
 
     def home(w, layer, d, half=2):
         p, q = place(layer)
@@ -115,13 +116,13 @@
             p, q = place(layer)
             for k, d, by in ((0, 2 - i, 1), (2, 3 - 3 * i, -1)):
                 source = terms[w].at[0, layer, rows(w, layer, p + 2, q + d)]
-                send(w, layer, 0, FAR + i, source, first[w].at[layer, k + i], to(layer, 0, by))
+                send(w, 0, FAR + i, source, first[w].at[layer, k + i], to(layer, 0, by))
 
         def g(layer, i):
             p, q = place(layer)
             for k, d, by, group in ((4, 3 - 3 * i, 1, NEAR + 1 + 2 * i), (6, 2 - i, -1, NEAR + i)):
                 source = terms[w].at[0, layer, rows(w, layer, p + by, q + d)]
-                send(w, layer, 0, group, source, first[w].at[layer, k + i], to(layer, 0, by))
+                send(w, 0, group, source, first[w].at[layer, k + i], to(layer, 0, by))
 
         over_layers(f, 2)
         over_layers(g, 2)
@@ -129,44 +130,44 @@
     def fwd1(w):
         take(own[w], load_sem.at[w])
         for i in range(2):
+            wait(w, FAR + i)
 
             def f(layer, i=i):
-                wait(w, layer, FAR + i)
                 for k, by, group in ((0, 1, NEAR + i), (2, -1, NEAR + 1 + 2 * i)):
                     add(w, layer, 2, k + i, (first[w], k + i))
-                    send(w, layer, 0, group, own[w].at[layer, k + i], first[w].at[layer, 8 + k + i], to(layer, 0, by))
+                    send(w, 0, group, own[w].at[layer, k + i], first[w].at[layer, 8 + k + i], to(layer, 0, by))
 
             over_layers(f)
 
     def send2(w, layer, slot, half, group, target, by):
         at = part(w, half)
-        send(w, layer, 1, group, own[w].at[layer, slot, at], second[w].at[layer, target, at], to(layer, 1, by))
+        send(w, 1, group, own[w].at[layer, slot, at], second[w].at[layer, target, at], to(layer, 1, by))
 
     def raw2(w):
         def f(layer):
-            wait(w, layer, NEAR)
             add(w, layer, 2, 6, (first[w], 8), (first[w], 6))
             send2(w, layer, 6, 0, FAR2, 0, 1)
             send2(w, layer, 6, 1, FAR2, 0, -1)
 
         def g(layer):
-            wait(w, layer, NEAR + 1)
             add(w, layer, 1, 5, (first[w], 9), (first[w], 7))
             send2(w, layer, 5, 1, LAST, 1, 1)
             add(w, layer, 0, 7, (first[w], 4), (first[w], 10))
             send2(w, layer, 7, 0, LAST, 2, -1)
 
+        wait(w, NEAR)
         over_layers(f)
+        wait(w, NEAR + 1)
         over_layers(g)
 
     def fwd2(w):
         def f(layer):
-            wait(w, layer, FAR2)
             add(w, layer, 0, 5, (first[w], 9), (first[w], 7), (second[w], 0))
             send2(w, layer, 5, 0, LAST, 1, 1)
             add(w, layer, 1, 7, (first[w], 4), (first[w], 10), (second[w], 0))
             send2(w, layer, 7, 1, LAST, 2, -1)
 
+        wait(w, FAR2)
         over_layers(f)
 
     def load_moments(w, layer):
@@ -181,6 +182,7 @@
         take(narrow[w], moment_sem.at[w, 1])
 
     def step(w):
+        wait(w, LAST)
         if w < 2:
             take_moments(w)
 
@@ -188,7 +190,6 @@
             slot = layer if w < 2 else 0
             if w == 2:
                 load_moments(w, layer)
-            wait(w, layer, LAST)
             if w == 2:
                 take_moments(w)
 
@@ -204,18 +205,18 @@
             blockwise(w, 2, one)
             for group, half, by in ((PARTS, 1, 1), (PARTS, 0, -1), (PARTS + 1, 0, 1), (PARTS + 1, 1, -1)):
                 source = second[w].at[layer, 1, part(w, half)]
-                send(w, layer, 2, group, source, home_there(w, layer, 0, by, half), to(layer, 1, by))
-            pltpu.make_async_copy(own[w].at[layer, 4], gs[w].at[layer], store_sem.at[w, 0]).start()
-            pltpu.make_async_copy(second[w].at[layer, 1], home(w, layer, 0), store_sem.at[w, 1]).start()
+                send(w, 2, group, source, home_there(w, layer, 0, by, half), to(layer, 1, by))
+            pltpu.make_async_copy(own[w].at[layer, 4], gs[w].at[layer], store_sem.at[w]).start()
+            pltpu.make_async_copy(second[w].at[layer, 1], home(w, layer, 0), store_sem.at[w]).start()
 
         over_layers(f, unroll=w == 2)
 
     def gather2(w):
         def f(layer):
-            wait(w, layer, PARTS)
             for half, by in ((1, 1), (0, -1)):
-                send(w, layer, 2, PARTS + 2, home(w, layer, -by, half), home_there(w, layer, -by, by, half), to(layer, 1, by))
-
+                send(w, 2, PARTS + 2, home(w, layer, -by, half), home_there(w, layer, -by, by, half), to(layer, 1, by))
+
+        wait(w, PARTS)
         over_layers(f, unroll=w == 2)
 
     def give(w, layer, d, source=None):
@@ -223,43 +224,40 @@
         for by in (1, -1):
             on = (by == 1) == (d % 2 == 0)
             if w < 2:
-                send(w, layer, 3, ON + d // 2 if on else REST, source, home(w, layer, d), to(layer, 0, by))
+                send(w, 3, ON + d // 2 if on else REST, source, home(w, layer, d), to(layer, 0, by))
             elif on:
-                send(w, layer, 3, REST, source, staged[2 * layer + d % 2].at[2 + d // 2], to(layer, 0, by))
+                send(w, 3, REST, source, staged[2 * layer + d % 2].at[2 + d // 2], to(layer, 0, by))
 
     def gather1(w):
         def f(layer):
-            give(w, layer, 0, second[w].at[layer, 1])
-            wait(w, layer, PARTS + 1)
             give(w, layer, 1)
             give(w, layer, 3)
 
+        over_layers(lambda layer: give(w, layer, 0, second[w].at[layer, 1]), unroll=w == 2)
+        wait(w, PARTS + 1)
         over_layers(f, unroll=w == 2)
 
     def gather1_far(w):
-        def f(layer):
-            wait(w, layer, PARTS + 2)
-            give(w, layer, 2)
-
-        over_layers(f, unroll=w == 2)
+        wait(w, PARTS + 2)
+        over_layers(lambda layer: give(w, layer, 2), unroll=w == 2)
 
     def gather1_on(w):
-        def f(layer, i):
-            p, q = place(layer)
-            wait(w, layer, ON + i, 2)
-            for d, by in ((2 * i, 1), (1 + 2 * i, -1)):
-                at = outs[w].at[layer, rows(w, layer, p - by, q + d)]
-                send(w, layer, 3, REST, at, at, to(layer, 0, by))
-
-        over_layers(f, 2)
+        for i in range(2):
+
+            def f(layer, i=i):
+                p, q = place(layer)
+                for d, by in ((2 * i, 1), (1 + 2 * i, -1)):
+                    at = outs[w].at[layer, rows(w, layer, p - by, q + d)]
+                    send(w, 3, REST, at, at, to(layer, 0, by))
+
+            wait(w, ON + i)
+            over_layers(f)
 
     def finish(w):
-        for layer in range(2):
-            wait(w, layer, REST, 4 if w == 2 else 8)
+        wait(w, REST, 4 if w == 2 else 8)
         for leg, ref in enumerate((first[w], second[w], second[w], own[w].at[0] if w == 2 else first[w])):
             take(ref, send_sem.at[w, leg])
-        for n in range(2):
-            take(gs[w], store_sem.at[w, n])
+        take(first[w].at[:, pl.ds(0, 2)], store_sem.at[w])
 
     raw1(0)
     loads(0)
@@ -379,7 +377,7 @@
         bf16, f32, dma = jnp.bfloat16, jnp.float32, pltpu.SemaphoreType.DMA
         anywhere = pl.BlockSpec(memory_space=pl.ANY)
 
-        def call(f, name, inputs, outputs, scratch, params, held=0, limit=LIMIT, **more):
+        def call(f, inputs, outputs, scratch, params, held=0, limit=LIMIT, **more):
             return pl.pallas_call(
                 f,
                 out_shape=[jax.ShapeDtypeStruct(one.shape, one.dtype) for one in outputs],
@@ -387,14 +385,13 @@
                 out_specs=[anywhere] * len(outputs),
                 scratch_shapes=scratch,
                 compiler_params=pltpu.CompilerParams(vmem_limit_bytes=limit, **params),
-                name=name,
                 **more,
             )(*inputs)
 
         scratch = [pltpu.VMEM((layers, count, *b), bf16) for count in (8, 12, 3) for b in blocks]
         scratch += [pltpu.VMEM((k, 2, *blocks[w]), f32) for w, k in ((0, layers), (2, 1))]
         scratch += [pltpu.VMEM((k, *blocks[w]), bf16) for w, k in ((0, layers), (2, 1))]
-        scratch += [dma((layers, len(BLOCKS)))] * 3 + [dma((3, 4)), dma((3,)), dma((3, 2)), dma((3, 2))]
+        scratch += [dma((3, len(BLOCKS))), dma((3, 4)), dma((3,)), dma((3, 2)), dma((3,))]
 
         def exchange(*refs):
             head, (wide, wide2, narrow, narrow2), sems = refs[:30], refs[30:34], refs[34:]
@@ -402,20 +399,22 @@
 
         stage = jax.ShapeDtypeStruct((side, *blocks[2]), bf16)
         g = [jax.ShapeDtypeStruct(one.shape, bf16) for one in m]
-        result = call(exchange, "exchange", arrays, [*weights[:2], *[stage] * 4, *g], scratch, {"collective_id": 0, "has_side_effects": True})
+        result = call(exchange, arrays, [*weights[:2], *[stage] * 4, *g], scratch, {"collective_id": 0, "has_side_effects": True})
         whole, staged, g = result[:2], result[2:6], result[6:]
-        brought = [lax.ppermute(one, "dp", on(n // 2, 1 - n % 2 * 2)) for n, one in enumerate(staged)]
+        brought = []
+        for n, one in enumerate(staged):
+            brought.append(lax.ppermute(one, "dp", on(n // 2, 1 - n % 2 * 2)))
 
         copied = [(layers, side, w.shape[1] // side, w.shape[2]) for w in weights[:2]] + [(layers, 2 * side, *blocks[2])]
         scratch = [pltpu.VMEM(one.shape, t) for t in (bf16, f32, f32) for one in m] + [pltpu.VMEM(shape, bf16) for shape in copied]
         scratch += [dma((3, 3)), dma((3, 2))] + [dma(shape[:2]) for shape in copied]
         cost = pl.CostEstimate(flops=18 * m[0].size, bytes_accessed=5 * weights[0].size, transcendentals=0)
-        result = call(functools.partial(settle, side), "settle", [*g, *m, *v, *whole, *staged], [*m, *v, *weights], scratch, {}, limit=LIMIT * 8 // 9, cost_estimate=cost)
+        result = call(functools.partial(settle, side), [*g, *m, *v, *whole, *staged], [*m, *v, *weights], scratch, {}, limit=LIMIT * 8 // 9, cost_estimate=cost)
         *moments, gate, up, down = result
         few = {"held": 2, "limit": LIMIT // 8, "input_output_aliases": {0: 0}}
         for layer in range(layers):
             inputs = [down, *brought[2 * layer : 2 * layer + 2]]
-            (down,) = call(functools.partial(patch, side, layer), "patch", inputs, [down], [dma((2, side))], {}, **few)
+            (down,) = call(functools.partial(patch, side, layer), inputs, [down], [dma((2, side))], {}, **few)
         return (gate, up, down, *moments)
 
     all_of, cut = P(None, None, None), P(None, "dp", None)

time: 428 us -> 428 us (level)
  no operation moved by 1% of the time
where the time goes in v1:
time: 428 us; the launch traced here: 427 us
  Pallas kernels  417 us (97%)
  starting transfers between devices  5.43 us (1%)
    pallas_call x4, Pallas kernels, call(): pl.pallas_call(f, out_shape=[jax.ShapeDtypeStruct(one.shape, one.dtype) f...  417 us
  transfers between devices with their start and end apart: 4, of which 2 were waited for; matrix products, arithmetic and copies ran while one was open for 0% of the time, Pallas kernels for 7%

profile of v1, /device:TPU:97, one launch (start us, length us, event | category | flops | bytes accessed | tf_op | source)
XLA Modules:
  0.0 426.9 jit_solution(12504734578475863015)
XLA Ops:
  0.6 383.5 %shard_map.187 = (bf16[2,1024,3328]{2,1,0:T(8,128)(2,1)}, bf16[2,1024,3328]{2,1,0:T(8,128)(2,1)}, bf16[4,208,1024]{2,1,0:T(8,128)(2,1)}, bf16[4,208,1024]{2,1,0:...) custom-call(bf16[1,2,1024,3328]{3,2,1,0:T(8,128)(2,1)} %refs_0_.1, ...), custom_call_target="tpu_custom_call" | custom-call | tf_op jit(solution)/shard_map/pallas_call | solution.py:381
  384.1 0.1 collective-permute-start
  384.3 2.7 collective-permute-start.1
  386.9 0.0 collective-permute-start.2
  386.9 2.7 collective-permute-start.3
  389.6 29.7 %shard_map.188 = (f32[2,64,3328]{2,1,0:T(8,128)}, f32[2,64,3328]{2,1,0:T(8,128)}, f32[2,208,1024]{2,1,0:T(8,128)}, f32[2,64,3328]{2,1,0:T(8,128)}, f32[2,64,3328...) custom-call(bf16[2,64,3328]{2,1,0:T(8,128)(2,1)} %get-tuple-element., ...), custom_call_target="tpu_custom_call" | custom-call | flops 7667712 | bytes 34078720 | tf_op jit(solution)/shard_map/pallas_call | solution.py:381
  419.3 3.6 collective-permute-done.refs_1_
  423.0 0.0 collective-permute-done.1.refs_2_
  423.0 1.8 shard_map.189.refs_0_
  424.8 0.3 collective-permute-done.2.refs_1_
  425.1 0.0 collective-permute-done.3.refs_2_
  425.1 1.8 shard_map.190
Async XLA Ops:
  384.1 38.8 %collective-permute-start = (bf16[4,208,1024]{2,1,0:T(8,128)(2,1)}, bf16[4,208,1024]{2,1,0:T(8,128)(2,1)S(1)}, u32[]{:S(2)}, u32[]{:S(2)}) collective-permute-start(bf16[4,208,1024]{2,1,0:T(8,128)(2,1)} %get-tuple-element.32.refs_11_), channel_id=1, source_target_pairs={{0,4},{1,5},{2,6},{3,7},{4,8},{5,9},{6,10},{7,11},{8,12},{9,13},{1... | collective-permute-start | bytes 5111816 | tf_op jit(solution)/shard_map/ppermute | solution.py:406
  384.3 38.7 %collective-permute-start.1 = (bf16[4,208,1024]{2,1,0:T(8,128)(2,1)}, bf16[4,208,1024]{2,1,0:T(8,128)(2,1)S(1)}, u32[]{:S(2)}, u32[]{:S(2)}) collective-permute-start(bf16[4,208,1024]{2,1,0:T(8,128)(2,1)} %get-tuple-element.33.refs_12_), channel_id=1, source_target_pairs={{0,12},{1,13},{2,14},{3,15},{4,0},{5,1},{6,2},{7,3},{8,4},{9,5},{1... | collective-permute-start | bytes 5111816 | tf_op jit(solution)/shard_map/ppermute | solution.py:406
  386.9 38.2 %collective-permute-start.2 = (bf16[4,208,1024]{2,1,0:T(8,128)(2,1)}, bf16[4,208,1024]{2,1,0:T(8,128)(2,1)S(1)}, u32[]{:S(2)}, u32[]{:S(2)}) collective-permute-start(bf16[4,208,1024]{2,1,0:T(8,128)(2,1)} %get-tuple-element.34.refs_13_), channel_id=1, source_target_pairs={{0,1},{1,2},{2,3},{3,0},{4,5},{5,6},{6,7},{7,4},{8,9},{9,10},{10,1... | collective-permute-start | bytes 5111816 | tf_op jit(solution)/shard_map/ppermute | solution.py:406
  386.9 38.2 %collective-permute-start.3 = (bf16[4,208,1024]{2,1,0:T(8,128)(2,1)}, bf16[4,208,1024]{2,1,0:T(8,128)(2,1)S(1)}, u32[]{:S(2)}, u32[]{:S(2)}) collective-permute-start(bf16[4,208,1024]{2,1,0:T(8,128)(2,1)} %get-tuple-element.35.refs_14_), channel_id=1, source_target_pairs={{0,3},{1,0},{2,1},{3,2},{4,7},{5,4},{6,5},{7,6},{8,11},{9,8},{10,9... | collective-permute-start | bytes 5111816 | tf_op jit(solution)/shard_map/ppermute | solution.py:406

commit v2 on v1

--- a/solution.py
+++ b/solution.py
@@ -133,8 +133,9 @@
             wait(w, FAR + i)
 
             def f(layer, i=i):
+                for k in (0, 2):
+                    add(w, layer, 2, k + i, (first[w], k + i))
                 for k, by, group in ((0, 1, NEAR + i), (2, -1, NEAR + 1 + 2 * i)):
-                    add(w, layer, 2, k + i, (first[w], k + i))
                     send(w, 0, group, own[w].at[layer, k + i], first[w].at[layer, 8 + k + i], to(layer, 0, by))
 
             over_layers(f)
@@ -151,8 +152,8 @@
 
         def g(layer):
             add(w, layer, 1, 5, (first[w], 9), (first[w], 7))
+            add(w, layer, 0, 7, (first[w], 4), (first[w], 10))
             send2(w, layer, 5, 1, LAST, 1, 1)
-            add(w, layer, 0, 7, (first[w], 4), (first[w], 10))
             send2(w, layer, 7, 0, LAST, 2, -1)
 
         wait(w, NEAR)
@@ -163,8 +164,8 @@
     def fwd2(w):
         def f(layer):
             add(w, layer, 0, 5, (first[w], 9), (first[w], 7), (second[w], 0))
+            add(w, layer, 1, 7, (first[w], 4), (first[w], 10), (second[w], 0))
             send2(w, layer, 5, 0, LAST, 1, 1)
-            add(w, layer, 1, 7, (first[w], 4), (first[w], 10), (second[w], 0))
             send2(w, layer, 7, 1, LAST, 2, -1)
 
         wait(w, FAR2)
@@ -290,8 +291,9 @@
     gather1(2)
     gather1_on(1)
     gather1_far(2)
-    for w in range(3):
-        finish(w)
+    finish(0)
+    finish(1)
+    finish(2)
 
 
 def spots(side, size, shift):

time: 428 us -> 428 us (level)
  no operation moved by 1% of the time
where the time goes in v2:
time: 428 us; the launch traced here: 427 us
  Pallas kernels  417 us (97%)
  starting transfers between devices  5.43 us (1%)
    pallas_call x4, Pallas kernels, call(): pl.pallas_call(f, out_shape=[jax.ShapeDtypeStruct(one.shape, one.dtype) f...  417 us
  transfers between devices with their start and end apart: 4, of which 2 were waited for; matrix products, arithmetic and copies ran while one was open for 0% of the time, Pallas kernels for 7%

profile of v2, /device:TPU:97, one launch (start us, length us, event | category | flops | bytes accessed | tf_op | source)
XLA Modules:
  0.0 426.9 jit_solution(2673965282406219443)
XLA Ops:
  0.6 383.5 %shard_map.187 = (bf16[2,1024,3328]{2,1,0:T(8,128)(2,1)}, bf16[2,1024,3328]{2,1,0:T(8,128)(2,1)}, bf16[4,208,1024]{2,1,0:T(8,128)(2,1)}, bf16[4,208,1024]{2,1,0:...) custom-call(bf16[1,2,1024,3328]{3,2,1,0:T(8,128)(2,1)} %refs_0_.1, ...), custom_call_target="tpu_custom_call" | custom-call | tf_op jit(solution)/shard_map/pallas_call | solution.py:383
  384.1 0.1 collective-permute-start
  384.3 2.7 collective-permute-start.1
  386.9 0.0 collective-permute-start.2
  386.9 2.7 collective-permute-start.3
  389.6 29.7 %shard_map.188 = (f32[2,64,3328]{2,1,0:T(8,128)}, f32[2,64,3328]{2,1,0:T(8,128)}, f32[2,208,1024]{2,1,0:T(8,128)}, f32[2,64,3328]{2,1,0:T(8,128)}, f32[2,64,3328...) custom-call(bf16[2,64,3328]{2,1,0:T(8,128)(2,1)} %get-tuple-element., ...), custom_call_target="tpu_custom_call" | custom-call | flops 7667712 | bytes 34078720 | tf_op jit(solution)/shard_map/pallas_call | solution.py:383
  419.3 3.6 collective-permute-done.refs_1_
  423.0 0.0 collective-permute-done.1.refs_2_
  423.0 1.8 shard_map.189.refs_0_
  424.8 0.3 collective-permute-done.2.refs_1_
  425.1 0.0 collective-permute-done.3.refs_2_
  425.1 1.8 shard_map.190
Async XLA Ops:
  384.1 38.8 %collective-permute-start = (bf16[4,208,1024]{2,1,0:T(8,128)(2,1)}, bf16[4,208,1024]{2,1,0:T(8,128)(2,1)S(1)}, u32[]{:S(2)}, u32[]{:S(2)}) collective-permute-start(bf16[4,208,1024]{2,1,0:T(8,128)(2,1)} %get-tuple-element.32.refs_11_), channel_id=1, source_target_pairs={{0,4},{1,5},{2,6},{3,7},{4,8},{5,9},{6,10},{7,11},{8,12},{9,13},{1... | collective-permute-start | bytes 5111816 | tf_op jit(solution)/shard_map/ppermute | solution.py:408
  384.3 38.7 %collective-permute-start.1 = (bf16[4,208,1024]{2,1,0:T(8,128)(2,1)}, bf16[4,208,1024]{2,1,0:T(8,128)(2,1)S(1)}, u32[]{:S(2)}, u32[]{:S(2)}) collective-permute-start(bf16[4,208,1024]{2,1,0:T(8,128)(2,1)} %get-tuple-element.33.refs_12_), channel_id=1, source_target_pairs={{0,12},{1,13},{2,14},{3,15},{4,0},{5,1},{6,2},{7,3},{8,4},{9,5},{1... | collective-permute-start | bytes 5111816 | tf_op jit(solution)/shard_map/ppermute | solution.py:408
  386.9 38.2 %collective-permute-start.2 = (bf16[4,208,1024]{2,1,0:T(8,128)(2,1)}, bf16[4,208,1024]{2,1,0:T(8,128)(2,1)S(1)}, u32[]{:S(2)}, u32[]{:S(2)}) collective-permute-start(bf16[4,208,1024]{2,1,0:T(8,128)(2,1)} %get-tuple-element.34.refs_13_), channel_id=1, source_target_pairs={{0,1},{1,2},{2,3},{3,0},{4,5},{5,6},{6,7},{7,4},{8,9},{9,10},{10,1... | collective-permute-start | bytes 5111816 | tf_op jit(solution)/shard_map/ppermute | solution.py:408
  386.9 38.2 %collective-permute-start.3 = (bf16[4,208,1024]{2,1,0:T(8,128)(2,1)}, bf16[4,208,1024]{2,1,0:T(8,128)(2,1)S(1)}, u32[]{:S(2)}, u32[]{:S(2)}) collective-permute-start(bf16[4,208,1024]{2,1,0:T(8,128)(2,1)} %get-tuple-element.35.refs_14_), channel_id=1, source_target_pairs={{0,3},{1,0},{2,1},{3,2},{4,7},{5,4},{6,5},{7,6},{8,11},{9,8},{10,9... | collective-permute-start | bytes 5111816 | tf_op jit(solution)/shard_map/ppermute | solution.py:408
